TPU v7x, 256 devices: a whole 4x4x8 slice. The times are simulated.
256 devices in a mesh: blk: 128 (over z_lo, y, x, core), rep: 2 (over z_hi).
Axes of the slice: x: 4, y: 4, z: 8 (z_hi: 2, z_lo: 4; z = z_hi * 4 + z_lo), core: 2. Of those that a mesh axis runs over, the one named last changes fastest.
Arguments:
- load_coef: bfloat16 [256, 2049, 256], P('blk', None, 'rep'), parts along dimension 2, may hold values from -0.29882812 to 0.29882812
- legendre: bfloat16 [256, 2049, 1024], P('blk'), may hold values from -0.125 to 0.125
- slab_orders: int32 [256], replicated, may hold values from 0 to 1023, as said below
- cycle_rows: int32 [1024], replicated, may hold values from 0 to 1023, each once
Outputs:
- potential: bfloat16 [1024, 128, 4096], P('blk', 'rep'), parts along dimension 1
- energy: float32 [128], P('rep'), parts along dimension 0
There are 2 independent parts, one for each index of `rep`. A program takes and returns all parts, laid end to end along the dimension named above; an argument that names none is the same for every part. Nothing has to cross between parts.
Inputs may be any that keep to these rules, and one draw needn't show every extreme that they name: `slab_orders`: values are distinct and below (2048) / 2. `cycle_rows`: each cycle appears once.
All inputs are finite; a program needn't handle non-finite values.
Results may differ from a plain program's by a relative error of at most 0.0055.
Values may be sent and summed in bfloat16 or wider, within the bound.
No kernel may reach another device: no remote copies, remote signals or barrier semaphores. Data moves between devices by JAX's collectives and lax.ppermute only.
A program may use at most 128 MiB of HBM per device.

v0:
```python
import math
import jax
import jax.numpy as jnp
from jax import lax
from jax.sharding import Mesh
from jax.sharding import PartitionSpec as P

NLON = 4096
BLK = ("blk_0", "blk_1", "blk_2", "blk_3")


def one_axis_at_a_time(x, axes):
    for axis in axes:
        x = lax.psum(x, axis)
    return x


def basis_rows(frequency):
    coarse_ids = jnp.arange(NLON // 64, dtype=jnp.int32) * 64
    fine_ids = jnp.arange(64, dtype=jnp.int32)
    scale = 2.0 * math.pi / NLON
    coarse_angles = (frequency[:, None] * coarse_ids[None, :] % NLON).astype(jnp.float32) * scale
    fine_angles = (frequency[:, None] * fine_ids[None, :] % NLON).astype(jnp.float32) * scale
    cos_coarse = jnp.cos(coarse_angles)[:, :, None]
    sin_coarse = jnp.sin(coarse_angles)[:, :, None]
    cos_fine = jnp.cos(fine_angles)[:, None, :]
    sin_fine = jnp.sin(fine_angles)[:, None, :]
    cosine = (cos_coarse * cos_fine - sin_coarse * sin_fine).reshape(frequency.shape[0], NLON)
    sine = (sin_coarse * cos_fine + cos_coarse * sin_fine).reshape(frequency.shape[0], NLON)
    factor = jnp.where(frequency == 0, 1.0, 2.0).astype(jnp.float32)[:, None]
    return ((factor * cosine).astype(jnp.bfloat16), (-factor * sine).astype(jnp.bfloat16))


def fourier(received, low_orders, degree):
    cos_lower, sin_lower = basis_rows(low_orders)
    cos_upper, sin_upper = basis_rows(degree - low_orders)
    fourier_basis = jnp.stack([cos_lower, sin_lower, cos_upper, sin_upper], axis=1)
    return jnp.einsum("rnsf,nsk->rfk", received, fourier_basis, preferred_element_type=jnp.float32)


def shards(load_coef, legendre, slab_orders, cycle_rows):
    blocks = lax.axis_size(BLK)
    position = lax.axis_index(BLK)
    pair_count = load_coef.shape[0]
    slab_rows = load_coef.shape[1]
    fields = load_coef.shape[2] // 2
    lat_count = legendre.shape[2]
    degree = slab_rows - 2
    my_orders = lax.dynamic_slice_in_dim(slab_orders, position * pair_count, pair_count)
    row_ids = jnp.arange(slab_rows, dtype=jnp.int32)
    spectra = []
    for pair_index in range(pair_count):
        in_lower = (row_ids < slab_rows - 1 - my_orders[pair_index])[:, None]
        pair_coef = load_coef[pair_index]
        nothing = jnp.zeros_like(pair_coef)
        stacked = jnp.concatenate(
            [jnp.where(in_lower, pair_coef, nothing), jnp.where(in_lower, nothing, pair_coef)],
            axis=1,
        )
        spectra.append(
            lax.dot_general(
                legendre[pair_index],
                stacked,
                (((0,), (0,)), ((), ())),
                preferred_element_type=jnp.float32,
            ).astype(jnp.bfloat16)
        )
    spectra = jnp.stack(spectra, axis=1).reshape(lat_count, pair_count, 4, fields)
    spectra = jnp.take(spectra, cycle_rows, axis=0)
    all_orders = slab_orders.reshape(blocks, pair_count)
    cycle_grid = fourier(
        lax.all_to_all(spectra, BLK, split_axis=0, concat_axis=1, tiled=True),
        low_orders=all_orders.reshape(-1),
        degree=degree,
    )
    partial_energy = jnp.sum(cycle_grid * cycle_grid, axis=(0, 2))
    summed = one_axis_at_a_time(partial_energy, BLK)
    energy = summed / (lat_count * NLON)
    return (cycle_grid.astype(jnp.bfloat16), energy)


def solution(mesh):
    split = Mesh(
        mesh.devices.reshape(4, 4, 4, 2, mesh.shape["rep"]),
        ("blk_0", "blk_1", "blk_2", "blk_3", "rep"),
    )
    in_specs = (P(BLK, None, "rep"), P(BLK, None, None), P(), P())
    out_specs = (P(BLK, "rep", None), P("rep"))
    return jax.shard_map(
        shards, mesh=split, in_specs=in_specs, out_specs=out_specs, check_vma=False
    )
```

profile of v0, /device:TPU:1, one launch (start us, length us, event | category | flops | bytes accessed | tf_op | source)
XLA Modules:
  0.0 158.2 jit_solution(1284161723024664103)
XLA Ops:
  0.6 0.7 fusion.45
  1.3 0.7 compare_and_fusion
  2.0 0.8 dynamic_slice.3
  2.8 0.6 fusion.53
  4.7 3.6 %fusion.52 = (bf16[1,2049,128]{2,0,1:T(2,128)(2,1)S(1)}, bf16[1,2049,128]{2,0,1:T(2,128)(2,1)S(1)}) fusion(bf16[2,2049,128]{2,0,1:T(2,128)(2,1)} %param.4), kind=kLoop, calls=%fused_computation.100 | loop fusion | bytes 2098176 | tf_op jit(solution)/shard_map/slice | solution.py:54
  8.3 17.4 %fusion.51 = (bf16[1,2049,1024]{2,0,1:T(2,128)(2,1)S(1)}, bf16[1,2049,1024]{2,0,1:T(2,128)(2,1)}) fusion(bf16[2,2049,1024]{2,0,1:T(2,128)(2,1)} %param.5), kind=kLoop, calls=%fused_computation.99 | loop fusion | bytes 16785408 | tf_op jit(solution)/shard_map/slice | solution.py:62
  25.7 1.9 %broadcast_select_fusion.2 = (bf16[2049,128]{1,0:T(8,128)(2,1)S(1)}, bf16[2049,128]{1,0:T(8,128)(2,1)S(1)}, bf16[2049,128]{1,0:T(8,128)(2,1)S(1)}, bf16[2049,128]{1,0:T(8,128)(2,1)S(1)}) fusion(pred[2049]{0:T(1024)(128)(4,1)S(1)} %iota_compare_fusion, bf16[1,2049,128]{2,0,1:T(2,128)(2,1)S(1)} %get-tuple-element.9, ...), kind=kLoop, calls=%fused_computation.39 | loop fusion | flops 1049088 | bytes 3151362 | tf_op jit(solution)/shard_map/jit(_where)/select_n | solution.py:57
  27.7 1.5 fusion.11
  29.2 0.7 copy.12
  29.9 4.9 %fusion.12 = bf16[256,1024]{1,0:T(8,128)(2,1)S(1)} fusion(bf16[1,2049,1024]{2,0,1:T(2,128)(2,1)} %get-tuple-element.3, bf16[2049,128]{1,0:T(8,128)(2,1)S(1)} %get-tuple-element.7, bf16[2049,128]{1,0:T(8,128)(2,1)S(1)} %get-tuple-element.6), kind=kOutput, calls=%fused_computation.29 | convolution fusion | flops 1076626432 | bytes 5769728 | tf_op jit(solution)/shard_map/dot_general | solution.py:61
  34.8 0.7 copy.13
  35.6 3.1 %pad_maximum_fusion = bf16[1024,2,4,64]{3,2,1,0:T(4,128)(2,1)} fusion(bf16[1024,1,4,64]{3,2,1,0:T(4,128)(2,1)S(1)} %copy.13, bf16[1024,1,4,64]{3,2,1,0:T(4,128)(2,1)S(1)} %copy.12), kind=kLoop, calls=%fused_computation.24 | loop fusion | flops 524288 | bytes 2097152 | tf_op jit(solution)/shard_map/stack | solution.py:68
  38.6 5.8 %gather_fusion = bf16[1024,2,4,64]{3,2,1,0:T(4,128)(2,1)S(1)} fusion(bf16[1024,2,4,64]{3,2,1,0:T(4,128)(2,1)} %pad_maximum_fusion, s32[1024]{0:T(1024)S(1)} %fusion.45), kind=kCustom, calls=%fused_computation | custom fusion | bytes 2101248 | tf_op jit(solution)/shard_map/jit(_take)/gather | solution.py:69
  44.5 0.0 copy-start.7
  44.5 4.5 %broadcast_select_fusion = bf16[1024,2,4,64]{3,2,1,0:T(4,128)(2,1)} fusion(bf16[1024,2,4,64]{3,2,1,0:T(4,128)(2,1)S(1)} %gather_fusion, pred[1024]{0:T(1024)(128)(4,1)S(1)} %compare_and_fusion), kind=kLoop, calls=%fused_computation.27 | loop fusion | flops 524288 | bytes 2098176 | tf_op jit(solution)/shard_map/jit(_take)/select_n | solution.py:69
  49.0 5.1 %reshape.541 = bf16[128,2,2048]{2,1,0:T(2,128)(2,1)} reshape(bf16[1024,2,4,64]{3,2,1,0:T(4,128)(2,1)} %broadcast_select_fusion) | data formatting | bytes 2097152
  54.0 13.8 %all-to-all-start = ((bf16[128,2,2048]{2,1,0:T(2,128)(2,1)}), bf16[128,2,2048]{2,1,0:T(2,128)(2,1)S(1)}, u32[]{:S(2)}, u32[]{:S(2)}) async-start(bf16[128,2,2048]{2,1,0:T(2,128)(2,1)} %reshape.541), calls=%async_computation | async-start | bytes 2097152 | tf_op jit(solution)/shard_map/all_to_all | solution.py:72
  67.9 0.0 copy-done.7
  67.9 1.1 fusion.44
  69.0 6.5 %multiply_subtract_fusion = (f32[256,64,64]{0,2,1:T(8,128)}, f32[256,64,64]{0,2,1:T(8,128)}, f32[256,64,64]{0,2,1:T(8,128)}, f32[256,64,64]{0,2,1:T(8,128)}) fusion(f32[256,64]{0,1:T(8,128)S(1)} %get-tuple-element.29, f32[256,64]{0,1:T(8,128)S(1)} %get-tuple-element.30, f32[256,64]{0,1:T(8,128)S(1)} %get-tuple-element.28, ...), kind=kLoop, calls=%fused_computation.19 | loop fusion | flops 12582912 | bytes 17301504 | tf_op jit(solution)/shard_map/sub | solution.py:28
  75.5 5.6 %copy.19 = f32[256,1,4096]{2,0,1:T(8,128)} copy(f32[256,1,4096]{0,2,1:T(8,128)} %bitcast.54) | data formatting | bytes 8388608 | tf_op jit(solution)/shard_map/add | solution.py:29
  81.1 5.6 %copy.18 = f32[256,1,4096]{2,0,1:T(8,128)} copy(f32[256,1,4096]{0,2,1:T(8,128)} %bitcast.53) | data formatting | bytes 8388608 | tf_op jit(solution)/shard_map/sub | solution.py:28
  86.7 5.6 %copy.17 = f32[256,1,4096]{2,0,1:T(8,128)} copy(f32[256,1,4096]{0,2,1:T(8,128)} %bitcast.52) | data formatting | bytes 8388608 | tf_op jit(solution)/shard_map/add | solution.py:29
  92.3 5.6 %copy.16 = f32[256,1,4096]{2,0,1:T(8,128)} copy(f32[256,1,4096]{0,2,1:T(8,128)} %bitcast.51) | data formatting | bytes 8388608 | tf_op jit(solution)/shard_map/sub | solution.py:28
  97.9 4.1 %multiply_convert_fusion = bf16[256,1,4096]{2,0,1:T(8,128)(2,1)} fusion(f32[256,1,4096]{2,0,1:T(8,128)} %copy.19, f32[256]{0:T(256)S(1)} %get-tuple-element.19), kind=kLoop, calls=%fused_computation.16 | loop fusion | flops 2097152 | bytes 6292480 | tf_op jit(solution)/shard_map/convert_element_type | solution.py:31
  102.1 0.0 copy-done.2
  102.1 1.8 %multiply_convert_fusion.1 = bf16[256,1,4096]{2,0,1:T(8,128)(2,1)} fusion(f32[256,1,4096]{2,0,1:T(8,128)S(1)} %copy-done.2, f32[256]{0:T(256)S(1)} %get-tuple-element.21), kind=kLoop, calls=%fused_computation.18 | loop fusion | flops 2097152 | bytes 6292480 | tf_op jit(solution)/shard_map/convert_element_type | solution.py:31
  103.9 1.1 copy-done.1
  105.0 1.8 %multiply_convert_fusion.2 = bf16[256,1,4096]{2,0,1:T(8,128)(2,1)} fusion(f32[256,1,4096]{2,0,1:T(8,128)S(1)} %copy-done.1, f32[256]{0:T(256)S(1)} %get-tuple-element.20), kind=kLoop, calls=%fused_computation.20 | loop fusion | flops 2097152 | bytes 6292480 | tf_op jit(solution)/shard_map/convert_element_type | solution.py:31
  106.8 0.0 copy-done
  106.8 1.8 %multiply_convert_fusion.3 = bf16[256,1,4096]{2,0,1:T(8,128)(2,1)} fusion(f32[256,1,4096]{2,0,1:T(8,128)S(1)} %copy-done, f32[256]{0:T(256)S(1)} %get-tuple-element.18), kind=kLoop, calls=%fused_computation.22 | loop fusion | flops 2097152 | bytes 6292480 | tf_op jit(solution)/shard_map/convert_element_type | solution.py:31
  108.5 0.0 all-to-all-done
  108.6 1.4 reshape.542
  109.9 0.0 copy-start.5
  110.0 0.0 copy-start.6
  110.0 0.3 copy.49
  110.3 0.6 copy.15
  110.8 0.7 copy-done.3
  111.5 0.6 copy-done.4
  112.2 0.6 copy-done.5
  112.8 0.6 copy-done.6
  113.4 7.7 %bitcast_convert_fusion = (bf16[8,64,4096]{2,1,0:T(8,128)(2,1)}, f32[8,64,4096,1]{2,1,3,0:T(8,128)S(1)}) fusion(bf16[256,1,4096]{2,0,1:T(8,128)(2,1)S(1)} %copy-done.3, bf16[256,1,4096]{2,0,1:T(8,128)(2,1)S(1)} %copy-done.4, bf16[256,1,4096]{2,0,1:T(8,128)(2,1)S(1)} %copy-done.5, bf16[256,1,4096]{2,0,1:T(8,128)(2,1)S(1)} %copy-done.6, ...), kind=kOutput, calls=%fused_computation.10 | convolution fusion | flops 4309647360 | bytes 22020096 | tf_op jit(solution)/shard_map/rnsf,nsk->rfk/dot_general | solution.py:38
  121.1 0.8 fusion.7
  121.9 10.3 %psum.28 = f32[64]{0:T(128)S(1)} all-reduce(f32[64]{0:T(128)S(1)} %fusion.7), channel_id=1, replica_groups=mesh['blk_0'=4,'blk_1'=4,'blk_2'=4,'blk_3'=2,'rep'=2] {'blk_0'}, use_global_device_ids=true, to_apply=%region_1.2 | all-reduce | flops 64 | bytes 512 | tf_op jit(solution)/shard_map/psum | solution.py:14
  132.1 8.6 %psum.29 = f32[64]{0:T(128)S(1)} all-reduce(f32[64]{0:T(128)S(1)} %psum.28), channel_id=1, replica_groups=mesh['blk_0'=4,'blk_1'=4,'blk_2'=4,'blk_3'=2,'rep'=2] {'blk_1'}, use_global_device_ids=true, to_apply=%region_2.3 | all-reduce | flops 64 | bytes 512 | tf_op jit(solution)/shard_map/psum | solution.py:14
  140.7 8.4 %psum.30 = f32[64]{0:T(128)S(1)} all-reduce(f32[64]{0:T(128)S(1)} %psum.29), channel_id=1, replica_groups=mesh['blk_0'=4,'blk_1'=4,'blk_2'=4,'blk_3'=2,'rep'=2] {'blk_2'}, use_global_device_ids=true, to_apply=%region_3.4 | all-reduce | flops 64 | bytes 512 | tf_op jit(solution)/shard_map/psum | solution.py:14
  149.1 8.5 %psum.31 = f32[64]{0:T(128)S(1)} all-reduce(f32[64]{0:T(128)S(1)} %psum.30), channel_id=1, replica_groups=mesh['blk_0'=4,'blk_1'=4,'blk_2'=4,'blk_3'=2,'rep'=2] {'blk_3'}, use_global_device_ids=true, to_apply=%region_4.5 | all-reduce | flops 64 | bytes 512 | tf_op jit(solution)/shard_map/psum | solution.py:14
  157.7 0.5 broadcast_multiply_fusion
  (10 shorter events, 0.0 us)
Async XLA Ops:
  44.5 23.4 %copy-start.7 = (s32[256]{0:T(256)S(1)}, s32[256]{0:T(256)}, u32[]{:S(2)}) copy-start(s32[256]{0:T(256)} %param.6) | copy-start | bytes 3076
  54.0 54.5 %all-to-all-start = ((bf16[128,2,2048]{2,1,0:T(2,128)(2,1)}), bf16[128,2,2048]{2,1,0:T(2,128)(2,1)S(1)}, u32[]{:S(2)}, u32[]{:S(2)}) async-start(bf16[128,2,2048]{2,1,0:T(2,128)(2,1)} %reshape.541), calls=%async_computation | async-start | bytes 2097152 | tf_op jit(solution)/shard_map/all_to_all | solution.py:72
  97.9 4.1 %copy-start.2 = (f32[256,1,4096]{2,0,1:T(8,128)S(1)}, f32[256,1,4096]{2,0,1:T(8,128)}, u32[]{:S(2)}) copy-start(f32[256,1,4096]{2,0,1:T(8,128)} %copy.18) | copy-start | bytes 12582916
  102.1 2.9 %copy-start.1 = (f32[256,1,4096]{2,0,1:T(8,128)S(1)}, f32[256,1,4096]{2,0,1:T(8,128)}, u32[]{:S(2)}) copy-start(f32[256,1,4096]{2,0,1:T(8,128)} %copy.17) | copy-start | bytes 12582916
  103.8 2.9 %copy-start = (f32[256,1,4096]{2,0,1:T(8,128)S(1)}, f32[256,1,4096]{2,0,1:T(8,128)}, u32[]{:S(2)}) copy-start(f32[256,1,4096]{2,0,1:T(8,128)} %copy.16) | copy-start | bytes 12582916
  109.9 1.6 %copy-start.3 = (bf16[256,1,4096]{2,0,1:T(8,128)(2,1)S(1)}, bf16[256,1,4096]{2,0,1:T(8,128)(2,1)}, u32[]{:S(2)}) copy-start(bf16[256,1,4096]{2,0,1:T(8,128)(2,1)} %multiply_convert_fusion) | copy-start | bytes 6291460
  109.9 2.2 %copy-start.4 = (bf16[256,1,4096]{2,0,1:T(8,128)(2,1)S(1)}, bf16[256,1,4096]{2,0,1:T(8,128)(2,1)}, u32[]{:S(2)}) copy-start(bf16[256,1,4096]{2,0,1:T(8,128)(2,1)} %multiply_convert_fusion.1) | copy-start | bytes 6291460
  109.9 2.8 %copy-start.5 = (bf16[256,1,4096]{2,0,1:T(8,128)(2,1)S(1)}, bf16[256,1,4096]{2,0,1:T(8,128)(2,1)}, u32[]{:S(2)}) copy-start(bf16[256,1,4096]{2,0,1:T(8,128)(2,1)} %multiply_convert_fusion.2) | copy-start | bytes 6291460
  110.0 3.4 %copy-start.6 = (bf16[256,1,4096]{2,0,1:T(8,128)(2,1)S(1)}, bf16[256,1,4096]{2,0,1:T(8,128)(2,1)}, u32[]{:S(2)}) copy-start(bf16[256,1,4096]{2,0,1:T(8,128)(2,1)} %multiply_convert_fusion.3) | copy-start | bytes 6291460
where the time goes:
time: 159 us; the launch traced here: 158 us
  local copies, waits for them, and re-layouts  63.1 us (40%)
  blocking collectives  35.8 us (23%)
  other arithmetic  29.2 us (18%)
  matrix products  14.1 us (9%)
  starting transfers between devices  13.8 us (9%)
  between operations  2.12 us (1%)
    psum x4, blocking collectives, one_axis_at_a_time(): x = lax.psum(x, axis)  35.8 us
    slice x1, local copies, waits for them, and re-layouts, shards(): legendre[pair_index]  17.4 us
    all_to_all x1, starting transfers between devices, shards(): lax.all_to_all(spectra, BLK, split_axis=0, concat_axis=1, tiled=True)  13.8 us
    add x2, local copies, waits for them, and re-layouts, basis_rows(): sin_coarse * cos_fine + cos_coarse * sin_fine  11.2 us
    sub x2, local copies, waits for them, and re-layouts, basis_rows(): cos_coarse * cos_fine - sin_coarse * sin_fine  11.2 us
    unnamed x18, local copies, waits for them, and re-layouts  10.2 us
    dot_general x1, matrix products, fourier(): jnp.einsum('rnsf,nsk->rfk', received, fourier_basis, preferred_element_ty...  7.67 us
    sub x1, other arithmetic, basis_rows(): cos_coarse * cos_fine - sin_coarse * sin_fine  6.49 us
  transfers between devices with their start and end apart: 1, of which 0 were waited for; matrix products, arithmetic and copies ran while one was open for 25% of the time, Pallas kernels for 0%

commit v1 on v0

--- a/solution.py
+++ b/solution.py
@@ -11,7 +11,7 @@
 
 def one_axis_at_a_time(x, axes):
     for axis in axes:
-        x = lax.psum(x, axis)
+        x = jnp.sum(lax.all_gather(x, axis), axis=0)
     return x
 
 

time: 159 us -> 166 us (1.044)
  local copies, waits for them, and re-layouts: 63.1 us -> 67 us
  between operations: 2.12 us -> 4.8 us
    psum x4 -> x0, blocking collectives: 35.8 us -> none  [one_axis_at_a_time(): x = lax.psum(x, axis)]
    unnamed x0 -> x4, blocking collectives: none -> 35.7 us
    unnamed x18 -> x38, local copies, waits for them, and re-layouts: 10.2 us -> 13.7 us
where the time goes in v1:
time: 166 us; the launch traced here: 165 us
  local copies, waits for them, and re-layouts  67 us (40%)
  blocking collectives  35.7 us (22%)
  other arithmetic  29.2 us (18%)
  matrix products  14.1 us (8%)
  starting transfers between devices  13.8 us (8%)
  between operations  4.8 us (3%)
    unnamed x4, blocking collectives  35.7 us
    slice x1, local copies, waits for them, and re-layouts, shards(): legendre[pair_index]  17.4 us
    all_to_all x1, starting transfers between devices, shards(): lax.all_to_all(spectra, BLK, split_axis=0, concat_axis=1, tiled=True)  13.8 us
    unnamed x38, local copies, waits for them, and re-layouts  13.7 us
    sub x2, local copies, waits for them, and re-layouts, basis_rows(): cos_coarse * cos_fine - sin_coarse * sin_fine  11.3 us
    add x2, local copies, waits for them, and re-layouts, basis_rows(): sin_coarse * cos_fine + cos_coarse * sin_fine  11.2 us
    dot_general x1, matrix products, fourier(): jnp.einsum('rnsf,nsk->rfk', received, fourier_basis, preferred_element_ty...  7.67 us
    sub x1, other arithmetic, basis_rows(): cos_coarse * cos_fine - sin_coarse * sin_fine  6.49 us
  transfers between devices with their start and end apart: 1, of which 0 were waited for; matrix products, arithmetic and copies ran while one was open for 25% of the time, Pallas kernels for 0%

profile of v1, /device:TPU:1, one launch (start us, length us, event | category | flops | bytes accessed | tf_op | source)
XLA Modules:
  0.0 164.7 jit_solution(10368791179644406463)
XLA Ops:
  0.6 0.7 fusion.45
  1.3 0.7 compare_and_fusion
  2.0 0.8 dynamic_slice.3
  2.8 0.6 fusion.53
  4.7 3.6 %fusion.52 = (bf16[1,2049,128]{2,0,1:T(2,128)(2,1)S(1)}, bf16[1,2049,128]{2,0,1:T(2,128)(2,1)S(1)}) fusion(bf16[2,2049,128]{2,0,1:T(2,128)(2,1)} %param.4), kind=kLoop, calls=%fused_computation.100 | loop fusion | bytes 2098176 | tf_op jit(solution)/shard_map/slice | solution.py:54
  8.3 17.4 %fusion.51 = (bf16[1,2049,1024]{2,0,1:T(2,128)(2,1)S(1)}, bf16[1,2049,1024]{2,0,1:T(2,128)(2,1)}) fusion(bf16[2,2049,1024]{2,0,1:T(2,128)(2,1)} %param.5), kind=kLoop, calls=%fused_computation.99 | loop fusion | bytes 16785408 | tf_op jit(solution)/shard_map/slice | solution.py:62
  25.7 1.9 %broadcast_select_fusion.2 = (bf16[2049,128]{1,0:T(8,128)(2,1)S(1)}, bf16[2049,128]{1,0:T(8,128)(2,1)S(1)}, bf16[2049,128]{1,0:T(8,128)(2,1)S(1)}, bf16[2049,128]{1,0:T(8,128)(2,1)S(1)}) fusion(pred[2049]{0:T(1024)(128)(4,1)S(1)} %iota_compare_fusion, bf16[1,2049,128]{2,0,1:T(2,128)(2,1)S(1)} %get-tuple-element.9, ...), kind=kLoop, calls=%fused_computation.39 | loop fusion | flops 1049088 | bytes 3151362 | tf_op jit(solution)/shard_map/jit(_where)/select_n | solution.py:57
  27.7 1.5 fusion.11
  29.2 0.7 copy.25
  29.9 4.9 %fusion.12 = bf16[256,1024]{1,0:T(8,128)(2,1)S(1)} fusion(bf16[1,2049,1024]{2,0,1:T(2,128)(2,1)} %get-tuple-element.3, bf16[2049,128]{1,0:T(8,128)(2,1)S(1)} %get-tuple-element.7, bf16[2049,128]{1,0:T(8,128)(2,1)S(1)} %get-tuple-element.6), kind=kOutput, calls=%fused_computation.29 | convolution fusion | flops 1076626432 | bytes 5769728 | tf_op jit(solution)/shard_map/dot_general | solution.py:61
  34.8 0.7 copy.26
  35.6 3.1 %pad_maximum_fusion = bf16[1024,2,4,64]{3,2,1,0:T(4,128)(2,1)} fusion(bf16[1024,1,4,64]{3,2,1,0:T(4,128)(2,1)S(1)} %copy.26, bf16[1024,1,4,64]{3,2,1,0:T(4,128)(2,1)S(1)} %copy.25), kind=kLoop, calls=%fused_computation.24 | loop fusion | flops 524288 | bytes 2097152 | tf_op jit(solution)/shard_map/stack | solution.py:68
  38.6 5.8 %gather_fusion = bf16[1024,2,4,64]{3,2,1,0:T(4,128)(2,1)S(1)} fusion(bf16[1024,2,4,64]{3,2,1,0:T(4,128)(2,1)} %pad_maximum_fusion, s32[1024]{0:T(1024)S(1)} %fusion.45), kind=kCustom, calls=%fused_computation | custom fusion | bytes 2101248 | tf_op jit(solution)/shard_map/jit(_take)/gather | solution.py:69
  44.5 4.5 %broadcast_select_fusion = bf16[1024,2,4,64]{3,2,1,0:T(4,128)(2,1)} fusion(bf16[1024,2,4,64]{3,2,1,0:T(4,128)(2,1)S(1)} %gather_fusion, pred[1024]{0:T(1024)(128)(4,1)S(1)} %compare_and_fusion), kind=kLoop, calls=%fused_computation.27 | loop fusion | flops 524288 | bytes 2098176 | tf_op jit(solution)/shard_map/jit(_take)/select_n | solution.py:69
  48.9 5.1 %reshape.565 = bf16[128,2,2048]{2,1,0:T(2,128)(2,1)} reshape(bf16[1024,2,4,64]{3,2,1,0:T(4,128)(2,1)} %broadcast_select_fusion) | data formatting | bytes 2097152
  54.1 13.8 %all-to-all-start = ((bf16[128,2,2048]{2,1,0:T(2,128)(2,1)}), bf16[128,2,2048]{2,1,0:T(2,128)(2,1)S(1)}, u32[]{:S(2)}, u32[]{:S(2)}) async-start(bf16[128,2,2048]{2,1,0:T(2,128)(2,1)} %reshape.565), calls=%async_computation | async-start | bytes 2097152 | tf_op jit(solution)/shard_map/all_to_all | solution.py:72
  67.9 1.1 fusion.44
  69.0 6.5 %multiply_subtract_fusion = (f32[256,64,64]{0,2,1:T(8,128)}, f32[256,64,64]{0,2,1:T(8,128)}, f32[256,64,64]{0,2,1:T(8,128)}, f32[256,64,64]{0,2,1:T(8,128)}) fusion(f32[256,64]{0,1:T(8,128)S(1)} %get-tuple-element.29, f32[256,64]{0,1:T(8,128)S(1)} %get-tuple-element.30, f32[256,64]{0,1:T(8,128)S(1)} %get-tuple-element.28, ...), kind=kLoop, calls=%fused_computation.19 | loop fusion | flops 12582912 | bytes 17301504 | tf_op jit(solution)/shard_map/sub | solution.py:28
  75.5 5.6 %copy.32 = f32[256,1,4096]{2,0,1:T(8,128)} copy(f32[256,1,4096]{0,2,1:T(8,128)} %bitcast.58) | data formatting | bytes 8388608 | tf_op jit(solution)/shard_map/add | solution.py:29
  81.1 5.6 %copy.31 = f32[256,1,4096]{2,0,1:T(8,128)} copy(f32[256,1,4096]{0,2,1:T(8,128)} %bitcast.57) | data formatting | bytes 8388608 | tf_op jit(solution)/shard_map/sub | solution.py:28
  86.7 5.6 %copy.30 = f32[256,1,4096]{2,0,1:T(8,128)} copy(f32[256,1,4096]{0,2,1:T(8,128)} %bitcast.56) | data formatting | bytes 8388608 | tf_op jit(solution)/shard_map/add | solution.py:29
  92.3 5.7 %copy.29 = f32[256,1,4096]{2,0,1:T(8,128)} copy(f32[256,1,4096]{0,2,1:T(8,128)} %bitcast.55) | data formatting | bytes 8388608 | tf_op jit(solution)/shard_map/sub | solution.py:28
  98.0 0.6 dynamic-slice
  98.6 0.6 dynamic-slice.1
  100.6 0.7 dynamic-slice.2
  102.0 0.6 dynamic-slice.3
  103.2 4.0 %multiply_convert_fusion = bf16[256,1,4096]{2,0,1:T(8,128)(2,1)} fusion(f32[256,1,4096]{2,0,1:T(8,128)} %copy.32, f32[256]{0:T(256)S(1)} %get-tuple-element.19), kind=kLoop, calls=%fused_computation.16 | loop fusion | flops 2097152 | bytes 6292480 | tf_op jit(solution)/shard_map/convert_element_type | solution.py:31
  107.2 1.8 %multiply_convert_fusion.1 = bf16[256,1,4096]{2,0,1:T(8,128)(2,1)} fusion(f32[256,1,4096]{2,0,1:T(8,128)S(1)} %copy-done.2, f32[256]{0:T(256)S(1)} %get-tuple-element.21), kind=kLoop, calls=%fused_computation.18 | loop fusion | flops 2097152 | bytes 6292480 | tf_op jit(solution)/shard_map/convert_element_type | solution.py:31
  109.0 1.1 copy-done.1
  110.2 1.8 %multiply_convert_fusion.2 = bf16[256,1,4096]{2,0,1:T(8,128)(2,1)} fusion(f32[256,1,4096]{2,0,1:T(8,128)S(1)} %copy-done.1, f32[256]{0:T(256)S(1)} %get-tuple-element.20), kind=kLoop, calls=%fused_computation.20 | loop fusion | flops 2097152 | bytes 6292480 | tf_op jit(solution)/shard_map/convert_element_type | solution.py:31
  112.0 1.8 %multiply_convert_fusion.3 = bf16[256,1,4096]{2,0,1:T(8,128)(2,1)} fusion(f32[256,1,4096]{2,0,1:T(8,128)S(1)} %copy-done, f32[256]{0:T(256)S(1)} %get-tuple-element.18), kind=kLoop, calls=%fused_computation.22 | loop fusion | flops 2097152 | bytes 6292480 | tf_op jit(solution)/shard_map/convert_element_type | solution.py:31
  113.7 1.4 reshape.566
  115.1 0.3 copy.62
  115.4 0.6 copy.28
  116.0 0.7 copy-done.3
  116.7 0.6 copy-done.4
  117.3 0.6 copy-done.5
  117.9 0.6 copy-done.6
  118.6 7.7 %bitcast_convert_fusion = (bf16[8,64,4096]{2,1,0:T(8,128)(2,1)}, f32[8,64,4096,1]{2,1,3,0:T(8,128)S(1)}) fusion(bf16[256,1,4096]{2,0,1:T(8,128)(2,1)S(1)} %copy-done.3, bf16[256,1,4096]{2,0,1:T(8,128)(2,1)S(1)} %copy-done.4, bf16[256,1,4096]{2,0,1:T(8,128)(2,1)S(1)} %copy-done.5, bf16[256,1,4096]{2,0,1:T(8,128)(2,1)S(1)} %copy-done.6, ...), kind=kOutput, calls=%fused_computation.10 | convolution fusion | flops 4309647360 | bytes 22020096 | tf_op jit(solution)/shard_map/rnsf,nsk->rfk/dot_general | solution.py:38
  126.2 0.8 fusion.7
  127.0 0.2 dynamic-update-slice
  127.3 10.3 %all-reduce = f32[256]{0:T(256)S(1)} all-reduce(f32[256]{0:T(256)S(1)} %dynamic-update-slice), channel_id=2, replica_groups=mesh['blk_0'=4,'blk_1'=4,'blk_2'=4,'blk_3'=2,'rep'=2] {'blk_0'}, use_global_device_ids=true, to_apply=%add | all-reduce | flops 256 | bytes 2048
  137.7 0.2 dynamic-update-slice.1
  137.9 8.5 %all-reduce.1 = f32[256]{0:T(256)S(1)} all-reduce(f32[256]{0:T(256)S(1)} %dynamic-update-slice.1), channel_id=3, replica_groups=mesh['blk_0'=4,'blk_1'=4,'blk_2'=4,'blk_3'=2,'rep'=2] {'blk_1'}, use_global_device_ids=true, to_apply=%add.1 | all-reduce | flops 256 | bytes 2048
  146.5 0.2 dynamic-update-slice.2
  146.8 8.4 %all-reduce.2 = f32[256]{0:T(256)S(1)} all-reduce(f32[256]{0:T(256)S(1)} %dynamic-update-slice.2), channel_id=4, replica_groups=mesh['blk_0'=4,'blk_1'=4,'blk_2'=4,'blk_3'=2,'rep'=2] {'blk_2'}, use_global_device_ids=true, to_apply=%add.2 | all-reduce | flops 256 | bytes 2048
  155.5 8.5 %all-reduce.3 = f32[128]{0:T(128)S(1)} all-reduce(f32[128]{0:T(128)S(1)} %dynamic-update-slice.3), channel_id=5, replica_groups=mesh['blk_0'=4,'blk_1'=4,'blk_2'=4,'blk_3'=2,'rep'=2] {'blk_3'}, use_global_device_ids=true, to_apply=%add.3 | all-reduce | flops 128 | bytes 1024
  164.2 0.5 broadcast_multiply_fusion
  (38 shorter events, 0.7 us)
Async XLA Ops:
  44.4 23.4 %copy-start.7 = (s32[256]{0:T(256)S(1)}, s32[256]{0:T(256)}, u32[]{:S(2)}) copy-start(s32[256]{0:T(256)} %param.6) | copy-start | bytes 3076
  54.1 59.6 %all-to-all-start = ((bf16[128,2,2048]{2,1,0:T(2,128)(2,1)}), bf16[128,2,2048]{2,1,0:T(2,128)(2,1)S(1)}, u32[]{:S(2)}, u32[]{:S(2)}) async-start(bf16[128,2,2048]{2,1,0:T(2,128)(2,1)} %reshape.565), calls=%async_computation | async-start | bytes 2097152 | tf_op jit(solution)/shard_map/all_to_all | solution.py:72
  92.3 5.7 %copy-start.11 = (u32[256]{0:T(256)S(1)}, u32[256]{0:T(256)}, u32[]{:S(2)}) copy-start(u32[256]{0:T(256)} %constant.97) | copy-start | bytes 3076
  92.3 6.3 %copy-start.10 = (u32[256]{0:T(256)S(1)}, u32[256]{0:T(256)}, u32[]{:S(2)}) copy-start(u32[256]{0:T(256)} %constant.102) | copy-start | bytes 3076
  92.3 8.3 %copy-start.9 = (u32[256]{0:T(256)S(1)}, u32[256]{0:T(256)}, u32[]{:S(2)}) copy-start(u32[256]{0:T(256)} %constant.107) | copy-start | bytes 3076
  92.3 9.6 %copy-start.8 = (u32[256]{0:T(256)S(1)}, u32[256]{0:T(256)}, u32[]{:S(2)}) copy-start(u32[256]{0:T(256)} %constant.112) | copy-start | bytes 3076
  98.0 9.2 %copy-start.2 = (f32[256,1,4096]{2,0,1:T(8,128)S(1)}, f32[256,1,4096]{2,0,1:T(8,128)}, u32[]{:S(2)}) copy-start(f32[256,1,4096]{2,0,1:T(8,128)} %copy.31) | copy-start | bytes 12582916
  107.2 2.9 %copy-start.1 = (f32[256,1,4096]{2,0,1:T(8,128)S(1)}, f32[256,1,4096]{2,0,1:T(8,128)}, u32[]{:S(2)}) copy-start(f32[256,1,4096]{2,0,1:T(8,128)} %copy.30) | copy-start | bytes 12582916
  109.0 2.9 %copy-start = (f32[256,1,4096]{2,0,1:T(8,128)S(1)}, f32[256,1,4096]{2,0,1:T(8,128)}, u32[]{:S(2)}) copy-start(f32[256,1,4096]{2,0,1:T(8,128)} %copy.29) | copy-start | bytes 12582916
  115.1 1.6 copy-start.3
  115.1 2.2 %copy-start.4 = (bf16[256,1,4096]{2,0,1:T(8,128)(2,1)S(1)}, bf16[256,1,4096]{2,0,1:T(8,128)(2,1)}, u32[]{:S(2)}) copy-start(bf16[256,1,4096]{2,0,1:T(8,128)(2,1)} %multiply_convert_fusion.1) | copy-start | bytes 6291460
  115.1 2.8 %copy-start.5 = (bf16[256,1,4096]{2,0,1:T(8,128)(2,1)S(1)}, bf16[256,1,4096]{2,0,1:T(8,128)(2,1)}, u32[]{:S(2)}) copy-start(bf16[256,1,4096]{2,0,1:T(8,128)(2,1)} %multiply_convert_fusion.2) | copy-start | bytes 6291460
  115.1 3.4 %copy-start.6 = (bf16[256,1,4096]{2,0,1:T(8,128)(2,1)S(1)}, bf16[256,1,4096]{2,0,1:T(8,128)(2,1)}, u32[]{:S(2)}) copy-start(bf16[256,1,4096]{2,0,1:T(8,128)(2,1)} %multiply_convert_fusion.3) | copy-start | bytes 6291460
